TPU v7x, 512 devices: a whole 4x4x16 slice. The times are simulated.
512 devices in a mesh: dp: 8 (over x, core), feat: 64 (over z, y).
Axes of the slice: x: 4, y: 4, z: 16, core: 2. Of those that a mesh axis runs over, the one named last changes fastest.
Arguments:
- feature_slab: float32 [4096, 28672], P('dp', 'feat'), may hold values from -200 to 200, as said below
- basis_start: float32 [28672, 256], P('feat'), may hold values from -0.03125 to 0.03125
Outputs:
- basis_out: float32 [28672, 256], P('feat')
Inputs may be any that keep to these rules, and one draw needn't show every extreme that they name: `feature_slab`: Real-valued entries; column scales differ over features and row scales over rows.
All inputs are finite; a program needn't handle non-finite values.
Results may differ from a plain program's by a relative error of at most 0.0015.
Values sent between devices are 32-bit elements; how exact they have to be, the bound alone decides.
No kernel may reach another device: no remote copies, remote signals or barrier semaphores. Data moves between devices by JAX's collectives and lax.ppermute only.
A program may use at most 64 MiB of HBM per device.

v0:
```python
import math

import jax
import jax.numpy as jnp
from jax import lax
from jax.sharding import Mesh
from jax.sharding import PartitionSpec as P

FF = 28672
NS_STEPS = 5
FEAT = ("feat_0", "feat_1")


coef_first = 3.4445
coef_second = -4.775
coef_third = 2.0315


def in_blocks(array, dim, peers):
    before, after = (array.shape[:dim], array.shape[dim + 1 :])
    return jnp.moveaxis(array.reshape(*before, peers, -1, *after), dim, 0)


def sum_at_owner(array, axis, dim):
    tiles = in_blocks(array, dim, lax.axis_size(axis))
    arrived = lax.all_to_all(tiles, axis, split_axis=0, concat_axis=0, tiled=True)
    return arrived.sum(axis=0)


def sum_by_axis(array, axes, dim):
    far, near = axes
    own = sum_at_owner(in_blocks(array, dim, lax.axis_size(far)), near, dim + 1)
    return jnp.sum(lax.all_to_all(own, far, 0, 0, tiled=True), axis=0)


def gathered_by_axis(array, axes, dim):
    for axis in reversed(axes):
        array = lax.all_gather(array, axis, axis=dim, tiled=True)
    return array


def filled_up(lines, peers):
    spare = -lines.shape[0] % peers
    if not spare:
        return lines
    return jnp.concatenate([lines, jnp.zeros((spare, *lines.shape[1:]), lines.dtype)])


def laid_out(tiles, dim):
    dims = list(tiles.shape[1:])
    dims[dim] *= tiles.shape[0]
    return jnp.moveaxis(tiles, 0, dim).reshape(dims)


def from_everyone(array, axis):
    peers = lax.axis_size(axis)
    return lax.all_to_all(
        jnp.broadcast_to(array[None], (peers, *array.shape)), axis, 0, 0, tiled=True
    )


def gathered_copies(array, axis, dim):
    return laid_out(from_everyone(array, axis), dim)


def nested_sum(array, axes):
    padded = filled_up(array, lax.axis_size(axes))
    whole = gathered_copies(sum_at_owner(padded, axes, 0), axes, 0)
    return lax.slice_in_dim(whole, 0, len(array)).reshape(array.shape)


def together(arrays, axis):
    line, at, gathered = (jnp.concatenate([a.reshape(-1) for a in arrays]), 0, [])
    so_far = nested_sum(line, axis)
    for a in arrays:
        gathered.append(so_far[at : at + a.size].reshape(a.shape))
        at += a.size
    return tuple(gathered)


def over_copies(array, axis):
    everything = from_everyone(array, axis)
    return jnp.sum(everything, axis=0)


def plain_dot(left, right):
    return jnp.dot(left, right, precision=lax.Precision.HIGHEST, preferred_element_type=jnp.float32)


def inner_dot(left, right):
    return lax.dot_general(
        left,
        right,
        (((0,), (0,)), ((), ())),
        precision=lax.Precision.HIGHEST,
        preferred_element_type=jnp.float32,
    )


def newton_schulz(matrix):
    polar_iter = matrix / jnp.sqrt(jnp.sum(matrix * matrix) + 1e-12)
    for step_index in range(NS_STEPS):
        square_part = plain_dot(polar_iter, polar_iter.T)
        mixed_part = coef_second * square_part + coef_third * plain_dot(square_part, square_part)
        polar_iter = coef_first * polar_iter + plain_dot(mixed_part, polar_iter)
    return polar_iter


def cholesky_inverse(gram_matrix):
    lower_factor = jnp.linalg.cholesky(gram_matrix)
    identity = jnp.eye(gram_matrix.shape[0], dtype=gram_matrix.dtype)
    return jax.scipy.linalg.solve_triangular(lower_factor, identity, lower=True)


def per_device(feature_slab, basis_start):
    basis = basis_start
    groups = lax.axis_size("dp")
    my_rows = sum_by_axis(plain_dot(feature_slab, basis), ("feat_0", "feat_1"), 0)
    power_image = inner_dot(feature_slab, gathered_by_axis(my_rows, FEAT, 0))
    gram_matrix, cross_terms = together(
        (inner_dot(power_image, power_image), inner_dot(basis, power_image)), FEAT
    )
    inverse = cholesky_inverse(gram_matrix)
    orthonormal = plain_dot(power_image, inverse.T)
    correlation = plain_dot(cross_terms, inverse.T)
    aligned = plain_dot(orthonormal, newton_schulz(correlation.T))
    basis = over_copies(aligned, "dp") / groups
    return basis * math.sqrt(FF)


def solution(mesh):
    torus = Mesh(mesh.devices.reshape(mesh.shape["dp"], 16, 4), ("dp", "feat_0", "feat_1"))
    return jax.shard_map(
        per_device,
        mesh=torus,
        in_specs=(P("dp", FEAT), P(FEAT, None)),
        out_specs=P(FEAT, None),
        check_vma=False,
    )
```

profile of v0, /device:TPU:1, one launch (start us, length us, event | category | flops | bytes accessed | tf_op | source)
XLA Modules:
  0.0 275.8 jit_solution(9813930142373680020)
XLA Ops:
  0.0 1.2 copy-done
  1.2 2.8 %fusion.19 = f32[512,256]{1,0:T(8,128)S(1)} fusion(f32[512,448]{0,1:T(8,128)S(1)} %copy-done, f32[448,256]{1,0:T(8,128)} %param.3), kind=kOutput, calls=%fused_computation.58 | convolution fusion | flops 704643072 | bytes 1900544 | tf_op jit(solution)/shard_map/dot_general | solution.py:87
  4.1 11.7 %all_to_all.30 = f32[4,16,8,256]{3,2,1,0:T(8,128)S(1)} all-to-all(f32[4,16,8,256]{3,2,1,0:T(8,128)S(1)} %bitcast.78), channel_id=1, replica_groups=mesh['dp'=8,'feat_0'=16,'feat_1'=4] {'feat_1'}, dimensions={0} | all-to-all | bytes 1048576 | tf_op jit(solution)/shard_map/all_to_all | solution.py:26
  15.8 28.4 %all_to_all.31 = f32[16,8,256]{2,1,0:T(8,128)S(1)} all-to-all(f32[16,8,256]{2,1,0:T(8,128)S(1)} %reduce_sum.45), channel_id=1, replica_groups=mesh['dp'=8,'feat_0'=16,'feat_1'=4] {'feat_0'}, dimensions={0} | all-to-all | bytes 262144 | tf_op jit(solution)/shard_map/all_to_all | solution.py:33
  44.2 9.1 %all_gather.6 = f32[32,256]{1,0:T(8,128)S(1)} all-gather(f32[8,256]{1,0:T(8,128)S(1)} %reduce_sum.46), channel_id=1, replica_groups=mesh['dp'=8,'feat_0'=16,'feat_1'=4] {'feat_1'}, dimensions={0}, use_global_device_ids=true | all-gather | bytes 40960 | tf_op jit(solution)/shard_map/all_gather | solution.py:38
  53.4 24.8 %all_gather.7 = f32[512,256]{1,0:T(8,128)S(1)} all-gather(f32[32,256]{1,0:T(8,128)S(1)} %all_gather.6), channel_id=1, replica_groups=mesh['dp'=8,'feat_0'=16,'feat_1'=4] {'feat_0'}, dimensions={0}, use_global_device_ids=true | all-gather | bytes 557056 | tf_op jit(solution)/shard_map/all_gather | solution.py:38
  78.1 0.9 fusion.20
  79.1 1.0 convolution_bitcast_fusion
  80.1 1.0 fusion.21
  81.4 0.5 copy.12
  81.9 29.1 %all_to_all.32 = f32[64,1,2048]{2,1,0:T(1,128)S(1)} all-to-all(f32[64,1,2048]{2,1,0:T(1,128)S(1)} %copy.12), channel_id=1, replica_groups=mesh['dp'=8,'feat_0'=16,'feat_1'=4] {'feat_0','feat_1'}, dimensions={0} | all-to-all | bytes 1048576 | tf_op jit(solution)/shard_map/all_to_all | solution.py:26
  111.1 0.3 reduce_sum.47
  111.4 1.1 broadcast_in_dim.6
  112.5 5.9 %all-to-all-start.3 = ((f32[64,1,2048]{2,1,0:T(1,128)}), f32[64,1,2048]{2,1,0:T(1,128)S(1)}, u32[]{:S(2)}, u32[]{:S(2)}) async-start(f32[64,1,2048]{2,1,0:T(1,128)} %broadcast_in_dim.6), calls=%async_computation.3 | async-start | bytes 1048576 | tf_op jit(solution)/shard_map/all_to_all | solution.py:57
  118.4 21.7 %all-to-all-done.3 = f32[64,1,2048]{2,1,0:T(1,128)S(1)} async-done(((f32[64,1,2048]{2,1,0:T(1,128)}), f32[64,1,2048]{2,1,0:T(1,128)S(1)}, u32[]{:S(2)}, u32[]{:S(2)}) %all-to-all-start.3) | async-done | bytes 524320 | tf_op jit(solution)/shard_map/all_to_all | solution.py:57
  140.1 1.3 slice_reduce_fusion
  141.7 11.7 %cholesky.50 = f32[128,128]{1,0:T(8,128)S(1)} custom-call(f32[128,128]{1,0:T(8,128)S(1)} %cholesky.118), custom_call_target="Cholesky" | custom-call | tf_op jit(solution)/shard_map/jit(cholesky)/cholesky | solution.py:110
  153.5 9.8 %custom-call.15 = f32[1,128,128]{1,2,0:T(8,128)S(1)} custom-call(f32[1,128,128]{2,1,0:T(8,128)S(1)} %get-tuple-element.28), custom_call_target="InvertDiagBlocksLowerTriangular" | custom-call | tf_op jit(solution)/shard_map/jit(cholesky)/cholesky | solution.py:110
  163.8 11.7 %cholesky.105 = f32[128,128]{1,0:T(8,128)S(1)} custom-call(f32[128,128]{1,0:T(8,128)S(1)} %convolution_subtract_fusion.1), custom_call_target="Cholesky" | custom-call | tf_op jit(solution)/shard_map/jit(cholesky)/cholesky | solution.py:110
  175.5 0.7 compare_reduce_fusion
  177.6 4.1 %while.1 = (s32[]{:T(128)}, f32[256,256]{1,0:T(8,128)S(1)}, s32[2,2]{1,0:T(2,128)S(1)}, f32[2,128,128]{2,1,0:T(8,128)S(1)}, s32[]{:T(128)}) while((s32[]{:T(128)}, f32[256,256]{1,0:T(8,128)S(1)}, s32[2,2]{1,0:T(2,128)S(1)}, f32[2,128,128]{2,1,0:T(8,128)S(1)}, s32[]{:T(128)}) %tuple.25), condition=%wide.while_cond, body=%wide.while_body.sunk | while | flops 2 | bytes 131189 | solution.py:112
  177.6 0.7 fusion.71
  178.3 1.3 bitcast_dynamic-update-slice_fusion.2
  179.7 0.7 fusion.71
  180.3 1.3 bitcast_dynamic-update-slice_fusion.2
  181.7 19.9 %custom-call.16 = f32[2,128,128]{1,2,0:T(8,128)S(1)} custom-call(f32[2,128,128]{2,1,0:T(8,128)S(1)} %get-tuple-element.12), custom_call_target="InvertDiagBlocksLowerTriangular" | custom-call | tf_op jit(solution)/shard_map/jit(_solve_triangular)/triangular_solve | solution.py:112
  202.5 0.6 fusion.7
  203.0 1.0 multiply_reduce_fusion
  204.7 0.4 fusion.10
  205.2 0.4 fusion.4
  205.6 0.4 convolution_add_fusion.4
  206.0 0.4 fusion.22
  206.4 0.4 fusion.3
  206.8 0.4 convolution_add_fusion.3
  207.2 0.4 fusion.23
  207.6 0.4 fusion.2
  208.0 0.4 convolution_add_fusion.2
  208.3 0.4 fusion.24
  208.8 0.4 fusion.1
  209.1 0.4 convolution_add_fusion.1
  209.5 0.4 fusion.25
  209.9 0.4 fusion
  210.3 0.4 convolution_add_fusion
  210.7 0.5 fusion.26
  211.3 0.3 broadcast_in_dim.7
  211.6 61.1 %all_to_all.33 = f32[8,448,256]{2,1,0:T(8,128)} all-to-all(f32[8,448,256]{2,1,0:T(8,128)S(1)} %broadcast_in_dim.7), channel_id=1, replica_groups=mesh['dp'=8,'feat_0'=16,'feat_1'=4] {'dp'}, dimensions={0} | all-to-all | bytes 7340032 | tf_op jit(solution)/shard_map/all_to_all | solution.py:57
  272.7 2.3 reduce_sum.49
  275.0 0.8 broadcast_multiply_fusion
  (30 shorter events, 2.2 us)
Async XLA Ops:
  0.0 1.2 copy-start
  0.0 79.1 %copy-start.1 = (f32[448,256]{1,0:T(8,128)S(1)}, f32[448,256]{1,0:T(8,128)}, u32[]{:S(2)}) copy-start(f32[448,256]{1,0:T(8,128)} %param.3) | copy-start | bytes 1376260
  112.5 27.6 %all-to-all-start.3 = ((f32[64,1,2048]{2,1,0:T(1,128)}), f32[64,1,2048]{2,1,0:T(1,128)S(1)}, u32[]{:S(2)}, u32[]{:S(2)}) async-start(f32[64,1,2048]{2,1,0:T(1,128)} %broadcast_in_dim.6), calls=%async_computation.3 | async-start | bytes 1048576 | tf_op jit(solution)/shard_map/all_to_all | solution.py:57
where the time goes:
time: 276 us
  blocking collectives  164 us (59%)
  other arithmetic  57.6 us (21%)
  waiting for transfers between devices  21.7 us (8%)
  matrix products  15.1 us (5%)
  local copies, waits for them, and re-layouts  9.01 us (3%)
  starting transfers between devices  5.92 us (2%)
    all_to_all x1, blocking collectives, from_everyone(): lax.all_to_all(jnp.broadcast_to(array[None], (peers, *array.shape)), axis...  61.1 us
    all_to_all x2, blocking collectives, sum_at_owner(): lax.all_to_all(tiles, axis, split_axis=0, concat_axis=0, tiled=True)  40.9 us
    another operation x6, other arithmetic, cholesky_inverse(): lower_factor = jnp.linalg.cholesky(gram_matrix)  34 us
    all_gather x2, blocking collectives, gathered_by_axis(): array = lax.all_gather(array, axis, axis=dim, tiled=True)  33.9 us
    all_to_all x1, blocking collectives, sum_by_axis(): return jnp.sum(lax.all_to_all(own, far, 0, 0, tiled=True), axis=0)  28.4 us
    all_to_all x1, waiting for transfers between devices, from_everyone(): lax.all_to_all(jnp.broadcast_to(array[None], (peers, *array.shape)), axis...  21.7 us
    another operation x3, other arithmetic, cholesky_inverse(): return jax.scipy.linalg.solve_triangular(lower_factor, identity, lower=True)  19.9 us
    dot_general x19, matrix products, plain_dot(): jnp.dot(left, right, precision=lax.Precision.HIGHEST, preferred_element_t...  10.8 us
  transfers between devices with their start and end apart: 1, of which 1 were waited for; matrix products, arithmetic and copies ran while one was open for 0% of the time, Pallas kernels for 0%

commit v1 on v0

v1 whole, which is shorter than its diff:
```python
import math

import jax
import jax.numpy as jnp
from jax import lax
from jax.sharding import Mesh
from jax.sharding import PartitionSpec as P

FF = 28672
NS_STEPS = 5
FEAT = ("z_hi", "z_lo", "y")
PLANE = ("z_lo", "y")
DP = ("x", "core")

coef_first = 3.4445
coef_second = -4.775
coef_third = 2.0315


def summed_tiles(array, axis):
    peers = lax.axis_size(axis)
    tiles = array.reshape(peers, -1, *array.shape[1:])
    return jnp.sum(lax.all_to_all(tiles, axis, 0, 0, tiled=True), axis=0)


def from_everyone(array, axis):
    peers = lax.axis_size(axis)
    return lax.all_to_all(
        jnp.broadcast_to(array[None], (peers, *array.shape)), axis, 0, 0, tiled=True
    )


def copied_tiles(array, axis):
    everything = from_everyone(array, axis)
    return everything.reshape(-1, *array.shape[1:])


def summed_copies(array, axis):
    return jnp.sum(from_everyone(array, axis), axis=0)


def plain_dot(left, right):
    return jnp.dot(left, right, precision=lax.Precision.HIGHEST, preferred_element_type=jnp.float32)


def inner_dot(left, right):
    return lax.dot_general(
        left,
        right,
        (((0,), (0,)), ((), ())),
        precision=lax.Precision.HIGHEST,
        preferred_element_type=jnp.float32,
    )


def newton_schulz(matrix):
    polar_iter = matrix / jnp.sqrt(jnp.sum(matrix * matrix) + 1e-12)
    for step_index in range(NS_STEPS):
        square_part = plain_dot(polar_iter, polar_iter.T)
        mixed_part = coef_second * square_part + coef_third * plain_dot(square_part, square_part)
        polar_iter = coef_first * polar_iter + plain_dot(mixed_part, polar_iter)
    return polar_iter


def cholesky_inverse(gram_matrix):
    lower_factor = jnp.linalg.cholesky(gram_matrix)
    identity = jnp.eye(gram_matrix.shape[0], dtype=gram_matrix.dtype)
    return jax.scipy.linalg.solve_triangular(lower_factor, identity, lower=True)


def projected_sum(part):
    own = summed_tiles(summed_tiles(part, "y"), "z_lo")
    own = summed_copies(own, "z_hi")
    return copied_tiles(copied_tiles(own, "z_lo"), "y")


def gram_sum(power_image):
    half = power_image.shape[1] // 2
    left, right = power_image[:, :half], power_image[:, half:]
    part = jnp.concatenate([inner_dot(left, left), inner_dot(right, left), inner_dot(right, right)])
    own = summed_copies(summed_tiles(part, PLANE), "z_hi")
    top, cross, low = jnp.split(copied_tiles(own, PLANE), 3)
    return jnp.concatenate(
        [jnp.concatenate([top, cross.T], axis=1), jnp.concatenate([cross, low], axis=1)]
    )


def per_device(feature_slab, basis_start):
    groups = lax.axis_size(DP)
    projected = projected_sum(plain_dot(feature_slab, basis_start))
    power_image = inner_dot(feature_slab, projected)
    cross_terms = inner_dot(projected, projected)
    inverse = cholesky_inverse(gram_sum(power_image))
    correlation = plain_dot(cross_terms, inverse.T)
    aligned = plain_dot(power_image, plain_dot(inverse.T, newton_schulz(correlation.T)))
    own = summed_tiles(summed_tiles(aligned, "core"), "x") * (math.sqrt(FF) / groups)
    return copied_tiles(copied_tiles(own, "x"), "core")


def solution(mesh):
    torus = Mesh(mesh.devices.reshape(4, 2, 4, 4, 4), (*DP, *FEAT))
    return jax.shard_map(
        per_device,
        mesh=torus,
        in_specs=(P(DP, FEAT), P(FEAT, None)),
        out_specs=P(FEAT, None),
        check_vma=False,
    )
```

time: 276 us -> 220 us (0.80)
  blocking collectives: 164 us -> 129 us
  waiting for transfers between devices: 21.7 us -> 7.1 us
  other arithmetic: 57.6 us -> 54.1 us
    all_gather x2 -> x0, blocking collectives: 33.9 us -> none  [gathered_by_axis(): array = lax.all_gather(array, axis, axis=dim, tiled=True)]
    all_to_all x1, waiting for transfers between devices: 21.7 us -> 7.1 us  [from_everyone(): lax.all_to_all(jnp.broadcast_to(array[None], (peers, *array.shape)), axis...]
    all_to_all x3 -> x5, blocking collectives: 69.3 us -> 59.7 us  [summed_tiles(): return jnp.sum(lax.all_to_all(tiles, axis, 0, 0, tiled=True), axis=0)]
    all_to_all x1 -> x6, blocking collectives: 61.1 us -> 69.3 us  [from_everyone(): lax.all_to_all(jnp.broadcast_to(array[None], (peers, *array.shape)), axis...]
where the time goes in v1:
time: 220 us; the launch traced here: 219 us
  blocking collectives  129 us (59%)
  other arithmetic  54.1 us (25%)
  matrix products  15.9 us (7%)
  waiting for transfers between devices  7.1 us (3%)
  local copies, waits for them, and re-layouts  7.04 us (3%)
  starting transfers between devices  3.7 us (2%)
  between operations  2.33 us (1%)
    all_to_all x6, blocking collectives, from_everyone(): lax.all_to_all(jnp.broadcast_to(array[None], (peers, *array.shape)), axis...  69.3 us
    all_to_all x5, blocking collectives, summed_tiles(): return jnp.sum(lax.all_to_all(tiles, axis, 0, 0, tiled=True), axis=0)  59.7 us
    another operation x6, other arithmetic, cholesky_inverse(): lower_factor = jnp.linalg.cholesky(gram_matrix)  33.9 us
    another operation x3, other arithmetic, cholesky_inverse(): return jax.scipy.linalg.solve_triangular(lower_factor, identity, lower=True)  19.9 us
    dot_general x19, matrix products, plain_dot(): jnp.dot(left, right, precision=lax.Precision.HIGHEST, preferred_element_t...  10.8 us
    all_to_all x1, waiting for transfers between devices, from_everyone(): lax.all_to_all(jnp.broadcast_to(array[None], (peers, *array.shape)), axis...  7.1 us
  transfers between devices with their start and end apart: 1, of which 1 were waited for; matrix products, arithmetic and copies ran while one was open for 0% of the time, Pallas kernels for 0%

profile of v1, /device:TPU:1, one launch (start us, length us, event | category | flops | bytes accessed | tf_op | source)
XLA Modules:
  0.0 219.2 jit_solution(9175810405919675306)
XLA Ops:
  0.0 1.2 copy-done
  1.2 2.8 %fusion.27 = f32[512,256]{1,0:T(8,128)S(1)} fusion(f32[512,448]{0,1:T(8,128)S(1)} %copy-done, f32[448,256]{1,0:T(8,128)} %param.3), kind=kOutput, calls=%fused_computation.65 | convolution fusion | flops 704643072 | bytes 1900544 | tf_op jit(solution)/shard_map/dot_general | solution.py:43
  4.0 11.7 %all_to_all.60 = f32[4,128,256]{2,1,0:T(8,128)S(1)} all-to-all(f32[4,128,256]{2,1,0:T(8,128)S(1)} %bitcast.86), channel_id=1, replica_groups=mesh['x'=4,'core'=2,'z_hi'=4,'z_lo'=4,'y'=4] {'y'}, dimensions={0} | all-to-all | bytes 1048576 | tf_op jit(solution)/shard_map/all_to_all | solution.py:23
  15.8 11.9 %all_to_all.61 = f32[4,32,256]{2,1,0:T(8,128)S(1)} all-to-all(f32[4,32,256]{2,1,0:T(8,128)S(1)} %bitcast.95), channel_id=1, replica_groups=mesh['x'=4,'core'=2,'z_hi'=4,'z_lo'=4,'y'=4] {'z_lo'}, dimensions={0} | all-to-all | bytes 262144 | tf_op jit(solution)/shard_map/all_to_all | solution.py:23
  27.7 24.0 %all_to_all.62 = f32[4,32,256]{2,1,0:T(8,128)S(1)} all-to-all(f32[4,32,256]{2,1,0:T(8,128)S(1)} %broadcast_in_dim.19), channel_id=1, replica_groups=mesh['x'=4,'core'=2,'z_hi'=4,'z_lo'=4,'y'=4] {'z_hi'}, dimensions={0} | all-to-all | bytes 262144 | tf_op jit(solution)/shard_map/all_to_all | solution.py:28
  51.8 7.4 %all_to_all.63 = f32[4,32,256]{2,1,0:T(8,128)S(1)} all-to-all(f32[4,32,256]{2,1,0:T(8,128)S(1)} %broadcast_in_dim.21), channel_id=1, replica_groups=mesh['x'=4,'core'=2,'z_hi'=4,'z_lo'=4,'y'=4] {'z_lo'}, dimensions={0} | all-to-all | bytes 262144 | tf_op jit(solution)/shard_map/all_to_all | solution.py:28
  59.3 9.3 %all_to_all.64 = f32[4,128,256]{2,1,0:T(8,128)S(1)} all-to-all(f32[4,128,256]{2,1,0:T(8,128)S(1)} %broadcast_in_dim.23), channel_id=1, replica_groups=mesh['x'=4,'core'=2,'z_hi'=4,'z_lo'=4,'y'=4] {'y'}, dimensions={0} | all-to-all | bytes 1048576 | tf_op jit(solution)/shard_map/all_to_all | solution.py:28
  68.6 0.9 fusion.28
  69.5 0.6 fusion.6
  70.1 0.6 fusion.8
  70.7 0.6 fusion.11
  71.3 11.4 %all_to_all.65 = f32[16,24,128]{2,1,0:T(8,128)S(1)} all-to-all(f32[16,24,128]{2,1,0:T(8,128)S(1)} %bitcast.93), channel_id=1, replica_groups=mesh['x'=4,'core'=2,'z_hi'=4,'z_lo'=4,'y'=4] {'z_lo','y'}, dimensions={0} | all-to-all | bytes 393216 | tf_op jit(solution)/shard_map/all_to_all | solution.py:23
  82.8 14.1 %all_to_all.66 = f32[4,24,128]{2,1,0:T(8,128)S(1)} all-to-all(f32[4,24,128]{2,1,0:T(8,128)S(1)} %broadcast_in_dim.24), channel_id=1, replica_groups=mesh['x'=4,'core'=2,'z_hi'=4,'z_lo'=4,'y'=4] {'z_hi'}, dimensions={0} | all-to-all | bytes 98304 | tf_op jit(solution)/shard_map/all_to_all | solution.py:28
  96.9 0.7 broadcast_in_dim.25
  97.6 3.7 %all-to-all-start.7 = ((f32[16,24,128]{2,1,0:T(8,128)}), f32[16,24,128]{2,1,0:T(8,128)S(1)}, u32[]{:S(2)}, u32[]{:S(2)}) async-start(f32[16,24,128]{2,1,0:T(8,128)} %broadcast_in_dim.25), calls=%async_computation.7 | async-start | bytes 393216 | tf_op jit(solution)/shard_map/all_to_all | solution.py:28
  101.3 1.0 convolution_bitcast_fusion
  102.4 7.1 %all-to-all-done.7 = f32[16,24,128]{2,1,0:T(8,128)S(1)} async-done(((f32[16,24,128]{2,1,0:T(8,128)}), f32[16,24,128]{2,1,0:T(8,128)S(1)}, u32[]{:S(2)}, u32[]{:S(2)}) %all-to-all-start.7) | async-done | bytes 196640 | tf_op jit(solution)/shard_map/all_to_all | solution.py:28
  110.0 11.7 %cholesky.50 = f32[128,128]{1,0:T(8,128)S(1)} custom-call(f32[128,128]{1,0:T(8,128)S(1)} %cholesky.118), custom_call_target="Cholesky" | custom-call | tf_op jit(solution)/shard_map/jit(cholesky)/cholesky | solution.py:66
  121.8 9.8 %custom-call.15 = f32[1,128,128]{1,2,0:T(8,128)S(1)} custom-call(f32[1,128,128]{2,1,0:T(8,128)S(1)} %get-tuple-element.29), custom_call_target="InvertDiagBlocksLowerTriangular" | custom-call | tf_op jit(solution)/shard_map/jit(cholesky)/cholesky | solution.py:66
  132.1 11.7 %cholesky.105 = f32[128,128]{1,0:T(8,128)S(1)} custom-call(f32[128,128]{1,0:T(8,128)S(1)} %convolution_subtract_fusion.1), custom_call_target="Cholesky" | custom-call | tf_op jit(solution)/shard_map/jit(cholesky)/cholesky | solution.py:66
  143.8 0.6 compare_reduce_fusion
  145.8 3.8 %while.1 = (s32[]{:T(128)}, f32[256,256]{1,0:T(8,128)S(1)}, s32[2,2]{1,0:T(2,128)S(1)}, f32[2,128,128]{2,1,0:T(8,128)S(1)}, s32[]{:T(128)}) while((s32[]{:T(128)}, f32[256,256]{1,0:T(8,128)S(1)}, s32[2,2]{1,0:T(2,128)S(1)}, f32[2,128,128]{2,1,0:T(8,128)S(1)}, s32[]{:T(128)}) %tuple.26), condition=%wide.while_cond, body=%wide.while_body.sunk | while | flops 2 | bytes 131189 | solution.py:68
  145.8 0.6 fusion.76
  146.4 1.3 bitcast_dynamic-update-slice_fusion.2
  147.7 0.6 fusion.76
  148.3 1.3 bitcast_dynamic-update-slice_fusion.2
  149.6 19.9 %custom-call.16 = f32[2,128,128]{1,2,0:T(8,128)S(1)} custom-call(f32[2,128,128]{2,1,0:T(8,128)S(1)} %get-tuple-element.12), custom_call_target="InvertDiagBlocksLowerTriangular" | custom-call | tf_op jit(solution)/shard_map/jit(_solve_triangular)/triangular_solve | solution.py:68
  170.4 1.0 multiply_reduce_fusion
  172.1 0.4 fusion.17
  172.5 0.4 fusion.4
  172.9 0.4 convolution_add_fusion.4
  173.3 0.4 fusion.29
  173.7 0.4 fusion.3
  174.1 0.4 convolution_add_fusion.3
  174.5 0.4 fusion.30
  174.9 0.4 fusion.2
  175.3 0.4 convolution_add_fusion.2
  175.7 0.4 fusion.31
  176.5 0.4 convolution_add_fusion.1
  176.9 0.4 fusion.32
  177.7 0.4 convolution_add_fusion
  178.1 0.6 fusion.13
  178.7 0.5 fusion.33
  179.2 15.4 %all_to_all.67 = f32[2,224,256]{2,1,0:T(8,128)S(1)} all-to-all(f32[2,224,256]{2,1,0:T(8,128)S(1)} %bitcast.87), channel_id=1, replica_groups=mesh['x'=4,'core'=2,'z_hi'=4,'z_lo'=4,'y'=4] {'core'}, dimensions={0} | all-to-all | bytes 917504 | tf_op jit(solution)/shard_map/all_to_all | solution.py:23
  194.7 9.3 %all_to_all.68 = f32[4,56,256]{2,1,0:T(8,128)S(1)} all-to-all(f32[4,56,256]{2,1,0:T(8,128)S(1)} %bitcast.90), channel_id=1, replica_groups=mesh['x'=4,'core'=2,'z_hi'=4,'z_lo'=4,'y'=4] {'x'}, dimensions={0} | all-to-all | bytes 458752 | tf_op jit(solution)/shard_map/all_to_all | solution.py:23
  204.0 7.7 %all_to_all.69 = f32[4,56,256]{2,1,0:T(8,128)S(1)} all-to-all(f32[4,56,256]{2,1,0:T(8,128)S(1)} %broadcast_in_dim.26), channel_id=1, replica_groups=mesh['x'=4,'core'=2,'z_hi'=4,'z_lo'=4,'y'=4] {'x'}, dimensions={0} | all-to-all | bytes 458752 | tf_op jit(solution)/shard_map/all_to_all | solution.py:28
  211.8 6.7 %all_to_all.70 = f32[2,224,256]{2,1,0:T(8,128)S(1)} all-to-all(f32[2,224,256]{2,1,0:T(8,128)S(1)} %broadcast_in_dim.54), channel_id=1, replica_groups=mesh['x'=4,'core'=2,'z_hi'=4,'z_lo'=4,'y'=4] {'core'}, dimensions={0} | all-to-all | bytes 917504 | tf_op jit(solution)/shard_map/all_to_all | solution.py:28
  218.5 0.8 copy.31
  (42 shorter events, 3.0 us)
Async XLA Ops:
  0.0 1.2 copy-start
  97.6 11.9 %all-to-all-start.7 = ((f32[16,24,128]{2,1,0:T(8,128)}), f32[16,24,128]{2,1,0:T(8,128)S(1)}, u32[]{:S(2)}, u32[]{:S(2)}) async-start(f32[16,24,128]{2,1,0:T(8,128)} %broadcast_in_dim.25), calls=%async_computation.7 | async-start | bytes 393216 | tf_op jit(solution)/shard_map/all_to_all | solution.py:28
